TPU v7x, 256 devices: a whole 4x4x8 slice. The times are simulated.
256 devices in a mesh: dp: 8 (over z), expert: 32 (over y, x, core).
Axes of the slice: x: 4, y: 4, z: 8, core: 2. Of those that a mesh axis runs over, the one named last changes fastest.
Arguments:
- tokens: bfloat16 [65536, 1280], P(('dp', 'expert')), may hold values from -14 to 14
- ln_gain: float32 [1280], replicated, may hold values from 0.25 to 1.75
- router: bfloat16 [1280, 32], replicated, may hold values from -0.3125 to 0.3125
- w_in: bfloat16 [32, 5120, 1280], P('expert', 'dp'), may hold values from -0.15625 to 0.15625
- b_in: bfloat16 [32, 5120], P('expert', 'dp'), may hold values from -3 to 3
- w_out: bfloat16 [32, 5120, 1280], P('expert', 'dp'), may hold values from -0.078125 to 0.078125
- b_out: bfloat16 [32, 1280], P('expert'), may hold values from -3 to 3
- expert_choice: int32 [65536], P(('dp', 'expert')), may hold values from 0 to 31
- modality: int32 [65536], P(('dp', 'expert')), may hold values from 0 to 1, as said below
- slot: int32 [65536], P(('dp', 'expert')), may hold values from -1 to 15, as said below
Outputs:
- moe_out: bfloat16 [65536, 1280], P(('dp', 'expert'))
- aux_losses: float32 [2, 2], replicated
Inputs may be any that keep to these rules, and one draw needn't show every extreme that they name: Each source's tokens with one expert and a slot other than -1 have distinct slots, numbered from 0 in token order; one expert has all 16 slots filled in every source. `modality`: every source holds tokens of both modalities.
All inputs are finite; a program needn't handle non-finite values.
Results may differ from a plain program's by a relative error of at most 0.007.
Values may be sent and summed in bfloat16 or wider, within the bound.
A program may use at most 128 MiB of HBM per device.

v0:
```python
import functools
import jax
import jax.numpy as jnp
from jax import lax
from jax.sharding import Mesh
from jax.sharding import PartitionSpec as P

CAP = 16
EXPERT = ("expert_0", "expert_1", "expert_2")
DP_EXPERT = ("dp", "expert_0", "expert_1", "expert_2")


def by_axis(x, axes):
    return functools.reduce(lax.psum, axes, x)


def layer_norm(tokens, ln_gain):
    values = tokens.astype(jnp.float32)
    center = values - jnp.mean(values, axis=-1, keepdims=True)
    spread = jnp.mean(center * center, axis=-1, keepdims=True)
    return (center * lax.rsqrt(spread + 1e-06) * ln_gain).astype(jnp.bfloat16)


def expert_hidden(rows, first, first_bias, second):
    pre = lax.dot_general(rows, first, (((1,), (1,)), ((), ())), preferred_element_type=jnp.float32)
    hidden = jax.nn.gelu(pre + first_bias.astype(jnp.float32), approximate=False).astype(
        jnp.bfloat16
    )
    return jnp.dot(hidden, second, preferred_element_type=jnp.float32)


def on_device(tokens, ln_gain, router, w_in, b_in, w_out, b_out, expert_choice, modality, slot):
    normed = layer_norm(tokens, ln_gain)
    logits = jnp.dot(normed, router, preferred_element_type=jnp.float32)
    logp = jax.nn.log_softmax(logits, axis=-1)
    probs = jnp.exp(logp)
    gate = jnp.take_along_axis(probs, expert_choice[:, None], axis=1)[:, 0]
    experts_all = router.shape[1]
    width = normed.shape[1]
    columns = experts_all * CAP
    target = jnp.where(slot >= 0, expert_choice * CAP + slot, -1)
    table = (target[:, None] == jnp.arange(columns, dtype=jnp.int32)[None, :]).astype(jnp.bfloat16)
    buffer = jnp.einsum("tk,td->kd", table, normed, preferred_element_type=jnp.float32).astype(
        jnp.bfloat16
    )
    received = lax.all_to_all(
        buffer.reshape(experts_all, CAP, width), EXPERT, split_axis=0, concat_axis=0, tiled=True
    )
    senders = lax.axis_size(EXPERT)
    local_count = w_in.shape[0]
    received = received.reshape(senders, local_count, CAP, width)
    rows = received[:, 0].reshape(senders * CAP, width)
    summed = expert_hidden(
        rows,
        lax.all_gather(w_in[0], "dp", axis=0, tiled=True),
        lax.all_gather(b_in[0], "dp", axis=0, tiled=True),
        lax.all_gather(w_out[0], "dp", axis=0, tiled=True),
    )
    results = [
        (summed + b_out[0].astype(jnp.float32)).astype(jnp.bfloat16).reshape(senders, CAP, width)
    ]
    outputs = jnp.stack(results, axis=1).reshape(experts_all, CAP, width)
    returned = lax.all_to_all(outputs, EXPERT, split_axis=0, concat_axis=0, tiled=True)
    fetched = jnp.dot(table, returned.reshape(columns, width), preferred_element_type=jnp.float32)
    moe_out = (gate[:, None] * fetched).astype(jnp.bfloat16)
    textual = (modality == 1).astype(jnp.float32)
    select = jnp.stack([1.0 - textual, textual], axis=0)
    entropy = -jnp.sum(probs * logp, axis=-1)
    prob_part = jnp.dot(select, probs, precision=lax.Precision.HIGHEST)
    ent_part = jnp.dot(select, entropy, precision=lax.Precision.HIGHEST)
    count_part = jnp.sum(select, axis=1)
    prob_sum, ent_sum, count = (
        by_axis(prob_part, DP_EXPERT),
        by_axis(ent_part, DP_EXPERT),
        by_axis(count_part, DP_EXPERT),
    )
    pbar = prob_sum / count[:, None]
    aux_losses = jnp.stack([ent_sum / count, jnp.sum(pbar * jnp.log(pbar), axis=1)], axis=1)
    return (moe_out, aux_losses)


def solution(mesh):
    finer = Mesh(
        mesh.devices.reshape(mesh.shape["dp"], 4, 4, 2), ("dp", "expert_0", "expert_1", "expert_2")
    )
    return jax.shard_map(
        on_device,
        mesh=finer,
        in_specs=(
            P(DP_EXPERT, None),
            P(),
            P(),
            P(EXPERT, "dp", None),
            P(EXPERT, "dp"),
            P(EXPERT, "dp", None),
            P(EXPERT, None),
            P(DP_EXPERT),
            P(DP_EXPERT),
            P(DP_EXPERT),
        ),
        out_specs=(P(DP_EXPERT, None), P()),
        check_vma=False,
    )
```

profile of v0, /device:TPU:1, one launch (start us, length us, event | category | flops | bytes accessed | tf_op | source)
XLA Modules:
  0.0 363.0 jit_solution(15232666370423474647)
XLA Ops:
  7.2 0.0 copy-start
  7.2 0.0 copy-start.4
  7.2 0.0 copy-start.1
  7.2 0.0 copy-start.2
  7.2 0.0 all-gather.6.cloned.1.call-start
  7.3 0.7 all-gather.6.cloned.1.call-update
  7.9 0.0 all-gather.8.cloned.1.call-start
  8.0 0.7 all-gather.8.cloned.1.call-update
  8.7 1.3 convert_reduce_fusion
  10.0 1.4 fusion.62
  11.4 0.7 compare_select_fusion
  12.1 2.9 convolution_convert_fusion
  15.0 8.6 %all-to-all-start = ((bf16[32,16,1280]{2,1,0:T(8,128)(2,1)}), bf16[32,16,1280]{2,1,0:T(8,128)(2,1)S(1)}, u32[]{:S(2)}, u32[]{:S(2)}) async-start(bf16[32,16,1280]{2,1,0:T(8,128)(2,1)} %bitcast.3), calls=%async_computation | async-start | bytes 2621440 | tf_op jit(solution)/shard_map/all_to_all | solution.py:46
  23.6 0.0 copy-done
  23.6 1.5 fusion.106
  25.2 0.0 copy-done.4
  25.2 25.4 %all-gather.1 = bf16[1,5120]{1,0:T(2,128)(2,1)S(1)} all-gather(bf16[1,640]{1,0:T(2,128)(2,1)S(1)} %copy-done.4), channel_id=3, replica_groups=mesh['dp'=8,'expert_0'=4,'expert_1'=4,'expert_2'=2] {'dp'}, dimensions={1}, use_global_device_ids=true | all-gather | bytes 11520 | tf_op jit(solution)/shard_map/all_gather | solution.py:56
  50.6 0.0 copy-done.1
  50.7 0.0 copy-done.2
  50.7 0.0 all-to-all-done
  50.7 101.4 %all-gather.6.cloned.1.call-done = bf16[1,5120,1280]{2,1,0:T(8,128)(2,1)} async-done(((bf16[1,640,1280]{2,1,0:T(8,128)(2,1)}), bf16[1,5120,1280]{2,1,0:T(8,128)(2,1)}) %all-gather.6.cloned.1.call-update) | async-done | bytes 13107216 | tf_op jit(solution)/shard_map/all_gather | solution.py:55
  152.1 31.7 %fusion.6.clone.8 = bf16[512,5120]{1,0:T(8,128)(2,1)} fusion(bf16[512,1280]{1,0:T(8,128)(2,1)S(1)} %bitcast.49, bf16[1,5120,1280]{2,1,0:T(8,128)(2,1)} %all-gather.6.cloned.1.call-done, f32[5120]{0:T(1024)S(1)} %bitcast.50), kind=kOutput, calls=%fused_computation.8.clone.clone.clone.clone.clone.clone.clone.1 | convolution fusion | flops 6883901440 | bytes 19681280 | tf_op jit(solution)/shard_map/dot_general | solution.py:25
  183.8 0.0 copy-start.3
  183.8 106.9 %all-gather.8.cloned.1.call-done = bf16[1,5120,1280]{2,1,0:T(8,128)(2,1)} async-done(((bf16[1,640,1280]{2,1,0:T(8,128)(2,1)}), bf16[1,5120,1280]{2,1,0:T(8,128)(2,1)}) %all-gather.8.cloned.1.call-update) | async-done | bytes 13107216 | tf_op jit(solution)/shard_map/all_gather | solution.py:57
  290.8 13.5 %fusion.54 = bf16[512,1280]{1,0:T(8,128)(2,1)} fusion(bf16[1,5120,1280]{2,1,0:T(8,128)(2,1)} %all-gather.8.cloned.1.call-done, f32[1280]{0:T(1024)S(1)} %convert_reduce_fusion.1, bf16[512,5120]{1,0:T(8,128)(2,1)} %fusion.6.clone.8), kind=kOutput, calls=%fused_computation.57 | convolution fusion | flops 6712197120 | bytes 19665920 | tf_op jit(solution)/shard_map/dot_general | solution.py:29
  304.2 7.7 %all-to-all-start.1 = ((bf16[32,16,1280]{2,1,0:T(8,128)(2,1)}), bf16[32,16,1280]{2,1,0:T(8,128)(2,1)S(1)}, u32[]{:S(2)}, u32[]{:S(2)}) async-start(bf16[32,16,1280]{2,1,0:T(8,128)(2,1)} %bitcast.8), calls=%async_computation.1 | async-start | bytes 2621440 | tf_op jit(solution)/shard_map/all_to_all | solution.py:63
  311.9 0.1 convolution_bitcast_fusion
  312.1 0.1 fusion.102
  312.2 0.1 fusion.67
  312.3 12.9 %all-reduce = (f32[2,32]{1,0:T(2,128)S(1)}, f32[2]{0:T(128)S(1)}, f32[2]{0:T(128)S(1)}) all-reduce(f32[2,32]{1,0:T(2,128)S(1)} %fusion.67, f32[2]{0:T(128)S(1)} %fusion.102, f32[2]{0:T(128)S(1)} %convolution_bitcast_fusion), channel_id=1, replica_groups=mesh['dp'=8,'expert_0'=4,'expert_1'=4,'expert_2'=2] {'dp'}, use_global_device_ids=true, to_apply=%region_14.15 | all-reduce | flops 68 | bytes 544 | tf_op jit(solution)/shard_map/psum | solution.py:14
  325.3 8.6 %all-reduce.2 = (f32[2,32]{1,0:T(2,128)S(1)}, f32[2]{0:T(128)S(1)}, f32[2]{0:T(128)S(1)}) all-reduce(f32[2,32]{1,0:T(2,128)S(1)} %get-tuple-element.8, f32[2]{0:T(128)S(1)} %get-tuple-element.9, f32[2]{0:T(128)S(1)} %get-tuple-element.10), channel_id=1, replica_groups=mesh['dp'=8,'expert_0'=4,'expert_1'=4,'expert_2'=2] {'expert_0'}, use_global_device_ids=true, to_apply=%region_15.16 | all-reduce | flops 68 | bytes 544 | tf_op jit(solution)/shard_map/psum | solution.py:14
  333.9 8.4 %all-reduce.1 = (f32[2,32]{1,0:T(2,128)S(1)}, f32[2]{0:T(128)S(1)}, f32[2]{0:T(128)S(1)}) all-reduce(f32[2,32]{1,0:T(2,128)S(1)} %get-tuple-element.14, f32[2]{0:T(128)S(1)} %get-tuple-element.15, f32[2]{0:T(128)S(1)} %get-tuple-element.16), channel_id=1, replica_groups=mesh['dp'=8,'expert_0'=4,'expert_1'=4,'expert_2'=2] {'expert_1'}, use_global_device_ids=true, to_apply=%region_16.17 | all-reduce | flops 68 | bytes 544 | tf_op jit(solution)/shard_map/psum | solution.py:14
  342.3 9.1 %all-reduce.3 = (f32[2,32]{1,0:T(2,128)S(1)}, f32[2]{0:T(128)S(1)}, f32[2]{0:T(128)S(1)}) all-reduce(f32[2,32]{1,0:T(2,128)S(1)} %get-tuple-element.11, f32[2]{0:T(128)S(1)} %get-tuple-element.12, f32[2]{0:T(128)S(1)} %get-tuple-element.13), channel_id=1, replica_groups=mesh['dp'=8,'expert_0'=4,'expert_1'=4,'expert_2'=2] {'expert_2'}, use_global_device_ids=true, to_apply=%region_17.18 | all-reduce | flops 68 | bytes 544 | tf_op jit(solution)/shard_map/psum | solution.py:14
  351.4 0.2 fusion.68
  351.6 0.7 copy.14
  352.3 2.4 gather_fusion
  354.7 0.0 copy-done.3
  354.7 0.0 all-to-all-done.1
  354.7 1.4 fusion.59
  (16 shorter events, 0.2 us)
Async XLA Ops:
  7.2 16.4 %copy-start = (bf16[1280,32]{0,1:T(8,128)(2,1)S(1)}, bf16[1280,32]{0,1:T(8,128)(2,1)}, u32[]{:S(2)}) copy-start(bf16[1280,32]{0,1:T(8,128)(2,1)} %param.12) | copy-start | bytes 245764
  7.2 18.0 %copy-start.4 = (bf16[1,640]{1,0:T(2,128)(2,1)S(1)}, bf16[1,640]{1,0:T(2,128)(2,1)}, u32[]{:S(2)}) copy-start(bf16[1,640]{1,0:T(2,128)(2,1)} %param.14) | copy-start | bytes 3844
  7.2 43.4 %copy-start.1 = (bf16[1,1280]{1,0:T(2,128)(2,1)S(1)}, bf16[1,1280]{1,0:T(2,128)(2,1)}, u32[]{:S(2)}) copy-start(bf16[1,1280]{1,0:T(2,128)(2,1)} %param.16) | copy-start | bytes 7684
  7.2 43.5 %copy-start.2 = (s32[256]{0:T(256)S(1)}, s32[256]{0:T(256)}, u32[]{:S(2)}) copy-start(s32[256]{0:T(256)} %param.18) | copy-start | bytes 3076
  7.2 144.9 %all-gather.6.cloned.1.call-start = ((), (), s32[]{:S(2)}) async-start(), calls=%async_computation.2 | async-start | bytes 14745600 | tf_op jit(solution)/shard_map/all_gather | solution.py:55
  7.9 282.8 %all-gather.8.cloned.1.call-start = ((), (), s32[]{:S(2)}) async-start(), calls=%async_computation.3 | async-start | bytes 14745600 | tf_op jit(solution)/shard_map/all_gather | solution.py:57
  15.0 35.7 %all-to-all-start = ((bf16[32,16,1280]{2,1,0:T(8,128)(2,1)}), bf16[32,16,1280]{2,1,0:T(8,128)(2,1)S(1)}, u32[]{:S(2)}, u32[]{:S(2)}) async-start(bf16[32,16,1280]{2,1,0:T(8,128)(2,1)} %bitcast.3), calls=%async_computation | async-start | bytes 2621440 | tf_op jit(solution)/shard_map/all_to_all | solution.py:46
  183.8 170.9 %copy-start.3 = (s32[256]{0:T(256)S(1)}, s32[256]{0:T(256)}, u32[]{:S(2)}) copy-start(s32[256]{0:T(256)} %param.17) | copy-start | bytes 3076
  304.2 50.5 %all-to-all-start.1 = ((bf16[32,16,1280]{2,1,0:T(8,128)(2,1)}), bf16[32,16,1280]{2,1,0:T(8,128)(2,1)S(1)}, u32[]{:S(2)}, u32[]{:S(2)}) async-start(bf16[32,16,1280]{2,1,0:T(8,128)(2,1)} %bitcast.8), calls=%async_computation.1 | async-start | bytes 2621440 | tf_op jit(solution)/shard_map/all_to_all | solution.py:63
Sparse Core Ops, SparseCore 0:
  9.8 142.2 all-gather.5
  153.9 136.8 all-gather.7
where the time goes:
time: 363 us
  waiting for transfers between devices  210 us (58%)
  blocking collectives  64.5 us (18%)
  matrix products  51.3 us (14%)
  starting transfers between devices  16.4 us (5%)
  between operations  14.2 us (4%)
  other arithmetic  3.85 us (1%)
    all_gather x1, waiting for transfers between devices, on_device(): lax.all_gather(w_out[0], 'dp', axis=0, tiled=True)  107 us
    all_gather x1, waiting for transfers between devices, on_device(): lax.all_gather(w_in[0], 'dp', axis=0, tiled=True)  101 us
    psum x4, blocking collectives, by_axis(): return functools.reduce(lax.psum, axes, x)  39.1 us
    dot_general x1, matrix products, expert_hidden(): lax.dot_general(rows, first, (((1,), (1,)), ((), ())), preferred_element_...  31.7 us
    all_gather x1, blocking collectives, on_device(): lax.all_gather(b_in[0], 'dp', axis=0, tiled=True)  25.4 us
    dot_general x1, matrix products, expert_hidden(): return jnp.dot(hidden, second, preferred_element_type=jnp.float32)  13.5 us
    all_to_all x1, starting transfers between devices, on_device(): lax.all_to_all(buffer.reshape(experts_all, CAP, width), EXPERT, split_axi...  8.58 us
    all_to_all x1, starting transfers between devices, on_device(): lax.all_to_all(outputs, EXPERT, split_axis=0, concat_axis=0, tiled=True)  7.7 us
  transfers between devices with their start and end apart: 4, of which 2 were waited for; matrix products, arithmetic and copies ran while one was open for 12% of the time, Pallas kernels for 0%

commit v1 on v0

--- a/solution.py
+++ b/solution.py
@@ -8,6 +8,11 @@
 CAP = 16
 EXPERT = ("expert_0", "expert_1", "expert_2")
 DP_EXPERT = ("dp", "expert_0", "expert_1", "expert_2")
+
+
+def exchange_gather(x, axis, dim):
+    sent = jnp.stack([x] * lax.axis_size(axis))
+    return jnp.concatenate(lax.all_to_all(sent, axis, 0, 0), axis=dim)
 
 
 def by_axis(x, axes):
@@ -52,7 +57,7 @@
     rows = received[:, 0].reshape(senders * CAP, width)
     summed = expert_hidden(
         rows,
-        lax.all_gather(w_in[0], "dp", axis=0, tiled=True),
+        exchange_gather(w_in[0], "dp", 0),
         lax.all_gather(b_in[0], "dp", axis=0, tiled=True),
         lax.all_gather(w_out[0], "dp", axis=0, tiled=True),
     )

time: 363 us -> 584 us (1.61)
  blocking collectives: 64.5 us -> 488 us
  waiting for transfers between devices: 210 us -> 0.69 us
  local copies, waits for them, and re-layouts: 3.06 us -> 10.1 us
    all_gather x1, blocking collectives: 25.4 us -> 418 us  [on_device(): lax.all_gather(b_in[0], 'dp', axis=0, tiled=True)]
    all_gather x1, waiting for transfers between devices: 107 us -> 0.01 us  [on_device(): lax.all_gather(w_out[0], 'dp', axis=0, tiled=True)]
    all_gather x1 -> x0, waiting for transfers between devices: 101 us -> none  [on_device(): lax.all_gather(w_in[0], 'dp', axis=0, tiled=True)]
    all_to_all x0 -> x1, blocking collectives: none -> 28.5 us  [on_device(): lax.all_to_all(buffer.reshape(experts_all, CAP, width), EXPERT, split_axi...]
    another operation x0 -> x1, local copies, waits for them, and re-layouts: none -> 7 us  [exchange_gather(): sent = jnp.stack([x] * lax.axis_size(axis))]
  transfers between devices with their start and end apart: 4 -> 3, of which waited for: 2 -> 0; matrix products, arithmetic and copies ran while one was open for 12% -> 6% of each run, Pallas kernels for 0% -> 0%
where the time goes in v1:
time: 584 us
  blocking collectives  488 us (84%)
  matrix products  49.2 us (8%)
  starting transfers between devices  17.8 us (3%)
  between operations  14.2 us (2%)
  local copies, waits for them, and re-layouts  10.1 us (2%)
    all_gather x1, blocking collectives, on_device(): lax.all_gather(b_in[0], 'dp', axis=0, tiled=True)  418 us
    psum x4, blocking collectives, by_axis(): return functools.reduce(lax.psum, axes, x)  41.2 us
    dot_general x1, matrix products, expert_hidden(): lax.dot_general(rows, first, (((1,), (1,)), ((), ())), preferred_element_...  31.8 us
    all_to_all x1, blocking collectives, on_device(): lax.all_to_all(buffer.reshape(experts_all, CAP, width), EXPERT, split_axi...  28.5 us
    dot_general x1, matrix products, expert_hidden(): return jnp.dot(hidden, second, preferred_element_type=jnp.float32)  13.5 us
  transfers between devices with their start and end apart: 3, of which 0 were waited for; matrix products, arithmetic and copies ran while one was open for 6% of the time, Pallas kernels for 0%

profile of v1, /device:TPU:1, one launch (start us, length us, event | category | flops | bytes accessed | tf_op | source)
XLA Modules:
  0.0 583.7 jit_solution(13066118093781119577)
XLA Ops:
  7.2 0.0 copy-start
  7.2 1.3 convert_reduce_fusion
  8.5 1.4 fusion.26
  9.9 0.7 compare_select_fusion
  10.6 1.9 convolution_convert_fusion
  12.5 28.5 %all_to_all.15 = bf16[32,16,1280]{2,1,0:T(8,128)(2,1)S(1)} all-to-all(bf16[32,16,1280]{2,1,0:T(8,128)(2,1)S(1)} %bitcast.43), channel_id=1, replica_groups=mesh['dp'=8,'expert_0'=4,'expert_1'=4,'expert_2'=2] {'expert_0','expert_..., dimensions={0} | all-to-all | bytes 2621440 | tf_op jit(solution)/shard_map/all_to_all | solution.py:51
  40.9 7.0 %stack.21 = bf16[8,640,1280]{2,1,0:T(8,128)(2,1)} broadcast(bf16[640,1280]{1,0:T(8,128)(2,1)} %bitcast.40), dimensions={1,2} | broadcast | bytes 14745600 | tf_op jit(solution)/shard_map/stack | solution.py:14
  47.9 0.0 copy-start.1
  47.9 0.0 copy-start.6
  47.9 0.0 copy-start.5
  47.9 0.0 copy-start.2
  47.9 0.0 copy-start.3
  48.0 8.3 %all-to-all-start.1 = ((bf16[8,640,1280]{2,1,0:T(8,128)(2,1)}), bf16[8,640,1280]{2,1,0:T(8,128)(2,1)}, u32[]{:S(2)}, u32[]{:S(2)}) async-start(bf16[8,640,1280]{2,1,0:T(8,128)(2,1)} %stack.21), calls=%async_computation.1 | async-start | bytes 26214400 | tf_op jit(solution)/shard_map/all_to_all | solution.py:15
  56.3 0.0 all-gather.4.cloned.1.call-start
  56.3 0.7 all-gather.4.cloned.1.call-update
  57.0 0.0 copy-done
  57.0 0.0 copy-done.1
  57.0 0.0 copy-done.6
  57.0 0.4 fusion.70
  57.6 0.0 copy-done.5
  57.6 418.2 %all-gather = bf16[1,5120]{1,0:T(2,128)(2,1)S(1)} all-gather(bf16[1,640]{1,0:T(2,128)(2,1)S(1)} %copy-done.5), channel_id=2, replica_groups=mesh['dp'=8,'expert_0'=4,'expert_1'=4,'expert_2'=2] {'dp'}, dimensions={1}, use_global_device_ids=true | all-gather | bytes 11520 | tf_op jit(solution)/shard_map/all_gather | solution.py:61
  475.8 0.0 copy-done.2
  475.9 0.0 copy-done.3
  475.9 0.0 all-to-all-done.1
  475.9 31.8 %fusion.4.clone.8 = bf16[512,5120]{1,0:T(8,128)(2,1)} fusion(bf16[512,1280]{1,0:T(8,128)(2,1)S(1)} %bitcast.42, bf16[5120,1280]{1,0:T(8,128)(2,1)} %bitcast.6, f32[5120]{0:T(1024)S(1)} %bitcast.44), kind=kOutput, calls=%fused_computation.6.clone.clone.clone.clone.clone.clone.clone.1 | convolution fusion | flops 6883901440 | bytes 19681280 | tf_op jit(solution)/shard_map/dot_general | solution.py:30
  507.7 0.0 copy-start.4
  507.7 0.0 all-gather.4.cloned.1.call-done
  507.7 13.5 %fusion.20 = bf16[512,1280]{1,0:T(8,128)(2,1)} fusion(bf16[1,5120,1280]{2,1,0:T(8,128)(2,1)} %all-gather.4.cloned.1.call-done, f32[1280]{0:T(1024)S(1)} %convert_reduce_fusion.1, bf16[512,5120]{1,0:T(8,128)(2,1)} %fusion.4.clone.8), kind=kOutput, calls=%fused_computation.29 | convolution fusion | flops 6712197120 | bytes 19665920 | tf_op jit(solution)/shard_map/dot_general | solution.py:34
  521.2 9.4 %all-to-all-start.2 = ((bf16[32,16,1280]{2,1,0:T(8,128)(2,1)}), bf16[32,16,1280]{2,1,0:T(8,128)(2,1)S(1)}, u32[]{:S(2)}, u32[]{:S(2)}) async-start(bf16[32,16,1280]{2,1,0:T(8,128)(2,1)} %bitcast.9), calls=%async_computation.2 | async-start | bytes 2621440 | tf_op jit(solution)/shard_map/all_to_all | solution.py:68
  530.6 0.1 convolution_bitcast_fusion
  530.7 0.1 fusion.66
  530.8 0.1 fusion.31
  531.0 14.9 %all-reduce = (f32[2,32]{1,0:T(2,128)S(1)}, f32[2]{0:T(128)S(1)}, f32[2]{0:T(128)S(1)}) all-reduce(f32[2,32]{1,0:T(2,128)S(1)} %fusion.31, f32[2]{0:T(128)S(1)} %fusion.66, f32[2]{0:T(128)S(1)} %convolution_bitcast_fusion), channel_id=1, replica_groups=mesh['dp'=8,'expert_0'=4,'expert_1'=4,'expert_2'=2] {'dp'}, use_global_device_ids=true, to_apply=%region_14.15 | all-reduce | flops 68 | bytes 544 | tf_op jit(solution)/shard_map/psum | solution.py:19
  545.9 8.7 %all-reduce.2 = (f32[2,32]{1,0:T(2,128)S(1)}, f32[2]{0:T(128)S(1)}, f32[2]{0:T(128)S(1)}) all-reduce(f32[2,32]{1,0:T(2,128)S(1)} %get-tuple-element.8, f32[2]{0:T(128)S(1)} %get-tuple-element.9, f32[2]{0:T(128)S(1)} %get-tuple-element.10), channel_id=1, replica_groups=mesh['dp'=8,'expert_0'=4,'expert_1'=4,'expert_2'=2] {'expert_0'}, use_global_device_ids=true, to_apply=%region_15.16 | all-reduce | flops 68 | bytes 544 | tf_op jit(solution)/shard_map/psum | solution.py:19
  554.6 8.4 %all-reduce.1 = (f32[2,32]{1,0:T(2,128)S(1)}, f32[2]{0:T(128)S(1)}, f32[2]{0:T(128)S(1)}) all-reduce(f32[2,32]{1,0:T(2,128)S(1)} %get-tuple-element.14, f32[2]{0:T(128)S(1)} %get-tuple-element.15, f32[2]{0:T(128)S(1)} %get-tuple-element.16), channel_id=1, replica_groups=mesh['dp'=8,'expert_0'=4,'expert_1'=4,'expert_2'=2] {'expert_1'}, use_global_device_ids=true, to_apply=%region_16.17 | all-reduce | flops 68 | bytes 544 | tf_op jit(solution)/shard_map/psum | solution.py:19
  563.0 9.1 %all-reduce.3 = (f32[2,32]{1,0:T(2,128)S(1)}, f32[2]{0:T(128)S(1)}, f32[2]{0:T(128)S(1)}) all-reduce(f32[2,32]{1,0:T(2,128)S(1)} %get-tuple-element.11, f32[2]{0:T(128)S(1)} %get-tuple-element.12, f32[2]{0:T(128)S(1)} %get-tuple-element.13), channel_id=1, replica_groups=mesh['dp'=8,'expert_0'=4,'expert_1'=4,'expert_2'=2] {'expert_2'}, use_global_device_ids=true, to_apply=%region_17.18 | all-reduce | flops 68 | bytes 544 | tf_op jit(solution)/shard_map/psum | solution.py:19
  572.1 0.2 fusion.32
  572.4 0.7 copy.14
  573.0 2.4 gather_fusion
  575.4 0.0 copy-done.4
  575.4 0.0 all-to-all-done.2
  575.5 1.4 fusion.23
  (16 shorter events, 0.2 us)
Async XLA Ops:
  7.2 49.9 %copy-start = (bf16[1280,32]{0,1:T(8,128)(2,1)S(1)}, bf16[1280,32]{0,1:T(8,128)(2,1)}, u32[]{:S(2)}) copy-start(bf16[1280,32]{0,1:T(8,128)(2,1)} %param.12) | copy-start | bytes 245764
  47.9 9.1 %copy-start.1 = (bf16[256,1280]{1,0:T(8,128)(2,1)S(1)}, bf16[256,1280]{1,0:T(8,128)(2,1)}, u32[]{:S(2)}) copy-start(bf16[256,1280]{1,0:T(8,128)(2,1)} %param.10) | copy-start | bytes 1966084
  47.9 9.1 %copy-start.6 = (f32[1280]{0:T(1024)S(1)}, f32[1280]{0:T(1024)}, u32[]{:S(2)}) copy-start(f32[1280]{0:T(1024)} %param.11) | copy-start | bytes 15364
  47.9 9.7 %copy-start.5 = (bf16[1,640]{1,0:T(2,128)(2,1)S(1)}, bf16[1,640]{1,0:T(2,128)(2,1)}, u32[]{:S(2)}) copy-start(bf16[1,640]{1,0:T(2,128)(2,1)} %param.14) | copy-start | bytes 3844
  47.9 427.9 %copy-start.2 = (bf16[1,1280]{1,0:T(2,128)(2,1)S(1)}, bf16[1,1280]{1,0:T(2,128)(2,1)}, u32[]{:S(2)}) copy-start(bf16[1,1280]{1,0:T(2,128)(2,1)} %param.16) | copy-start | bytes 7684
  47.9 427.9 %copy-start.3 = (s32[256]{0:T(256)S(1)}, s32[256]{0:T(256)}, u32[]{:S(2)}) copy-start(s32[256]{0:T(256)} %param.18) | copy-start | bytes 3076
  48.0 427.9 %all-to-all-start.1 = ((bf16[8,640,1280]{2,1,0:T(8,128)(2,1)}), bf16[8,640,1280]{2,1,0:T(8,128)(2,1)}, u32[]{:S(2)}, u32[]{:S(2)}) async-start(bf16[8,640,1280]{2,1,0:T(8,128)(2,1)} %stack.21), calls=%async_computation.1 | async-start | bytes 26214400 | tf_op jit(solution)/shard_map/all_to_all | solution.py:15
  56.3 451.4 %all-gather.4.cloned.1.call-start = ((), (), s32[]{:S(2)}) async-start(), calls=%async_computation.3 | async-start | bytes 14745600 | tf_op jit(solution)/shard_map/all_gather | solution.py:62
  507.7 67.8 %copy-start.4 = (s32[256]{0:T(256)S(1)}, s32[256]{0:T(256)}, u32[]{:S(2)}) copy-start(s32[256]{0:T(256)} %param.17) | copy-start | bytes 3076
  521.2 54.3 %all-to-all-start.2 = ((bf16[32,16,1280]{2,1,0:T(8,128)(2,1)}), bf16[32,16,1280]{2,1,0:T(8,128)(2,1)S(1)}, u32[]{:S(2)}, u32[]{:S(2)}) async-start(bf16[32,16,1280]{2,1,0:T(8,128)(2,1)} %bitcast.9), calls=%async_computation.2 | async-start | bytes 2621440 | tf_op jit(solution)/shard_map/all_to_all | solution.py:68
Sparse Core Ops, SparseCore 0:
  58.9 404.5 all-gather.3
